TPU v7x, 32 devices: a whole 2x2x4 slice. The times are simulated.
32 devices in a mesh: ta: 2 (over core), gx: 16 (over z, y, x).
Axes of the slice: x: 2, y: 2, z: 4, core: 2. Of those that a mesh axis runs over, the one named last changes fastest.
Arguments:
- time_links: float32 [6, 2, 3, 3, 96, 4608], P('ta', None, None, None, 'gx'), may hold values from -1 to 1, as said below
Outputs:
- loop_planes: float32 [96, 2, 4608], P('gx', None, 'ta')
- correlator: float32 [96, 49], P('gx')
Inputs may be any that keep to these rules, and one draw needn't show every extreme that they name: At every site and time, the matrix time_links[t, 0] + i time_links[t, 1] is special unitary.
All inputs are finite; a program needn't handle non-finite values.
Results may differ from a plain program's by a relative error of at most 0.00029.
Values sent between devices are 32-bit elements; how exact they have to be, the bound alone decides.
A program may use at most 64 MiB of HBM per device.

v0:
```python
import jax
import jax.numpy as jnp
from jax import lax
from jax.sharding import PartitionSpec as P


def prefix(value, axis, join, neutral):
    count, mine = (lax.axis_size(axis), lax.axis_index(axis))
    pieces = lax.all_gather(value, axis)
    subtotal = jnp.full_like(value, 0) + jnp.asarray(neutral, value.dtype)

    def step(position, subtotal):
        longer = join(subtotal, pieces[position])
        return jnp.where(position < mine, longer, subtotal)

    return lax.fori_loop(0, count - 1, step, subtotal)


def spread(value, axis, source):
    kept = jnp.where(lax.axis_index(axis) == source, value, 0).astype(value.dtype)
    return lax.psum(kept, axis)


def complex_mul(left, right):
    terms_real = []
    terms_imag = []
    for middle in range(3):
        left_real = left[0][:, middle : middle + 1]
        left_imag = left[1][:, middle : middle + 1]
        right_real = right[0][middle : middle + 1]
        right_imag = right[1][middle : middle + 1]
        terms_real.append(left_real * right_real - left_imag * right_imag)
        terms_imag.append(left_real * right_imag + left_imag * right_real)
    return jnp.stack(
        [
            terms_real[0] + terms_real[1] + terms_real[2],
            terms_imag[0] + terms_imag[1] + terms_imag[2],
        ]
    )


def trace_third(matrix):
    return (matrix[:, 0, 0] + matrix[:, 1, 1] + matrix[:, 2, 2]) / 3.0


def correlation(own_rows, others):
    return lax.dot_general(
        own_rows,
        others,
        (((1,), (1,)), ((), ())),
        precision=lax.Precision.HIGHEST,
        preferred_element_type=jnp.float32,
    )


def by_separation(products, offset, longest, period):
    row_index = lax.broadcasted_iota(jnp.int32, products.shape, 0)
    column_index = lax.broadcasted_iota(jnp.int32, products.shape, 1)
    separation = offset + column_index - row_index
    separation = separation % period
    targets = jnp.arange(longest + 1, dtype=jnp.int32)
    selector = (separation[:, :, None] == targets).astype(jnp.float32)
    return jnp.sum(products[:, :, None] * selector, axis=1)


def per_device(time_links):
    local_product = time_links[0]
    for slice_index in range(1, time_links.shape[0]):
        local_product = complex_mul(local_product, time_links[slice_index])
    plane_sites = time_links.shape[-1]
    ta_count = lax.axis_size("ta")
    site_share = plane_sites // ta_count
    unit_matrix = jnp.broadcast_to(
        jnp.eye(3, dtype=jnp.float32)[:, :, None, None], local_product.shape[1:]
    )
    identity = jnp.stack([unit_matrix, jnp.zeros_like(unit_matrix)])
    earlier = prefix(local_product, "ta", complex_mul, identity)
    full_product = complex_mul(earlier, local_product)
    traces = spread(trace_third(full_product), "ta", ta_count - 1)
    own_share = lax.dynamic_slice_in_dim(traces, lax.axis_index("ta") * site_share, site_share, 2)
    loop_planes = jnp.transpose(own_share, (1, 0, 2))
    planes = loop_planes.shape[0]
    flat_width = loop_planes.shape[1] * loop_planes.shape[2]
    gx_count = lax.axis_size("gx")
    far_blocks = gx_count // 2
    longest = planes * far_blocks
    own_rows = loop_planes.reshape(planes, flat_width)
    shard_rows = lax.all_gather(loop_planes, "gx", axis=0, tiled=True)
    products = correlation(own_rows, shard_rows.reshape(shard_rows.shape[0], flat_width))
    totals_part = by_separation(
        products, -lax.axis_index("gx") * planes, longest, planes * gx_count
    )
    correlator = lax.psum(totals_part, "ta") / plane_sites
    return (loop_planes, correlator)


def solution(mesh):
    in_specs = (P("ta", None, None, None, "gx", None),)
    out_specs = (P("gx", None, "ta"), P("gx", None))
    return jax.shard_map(
        per_device, mesh=mesh, in_specs=in_specs, out_specs=out_specs, check_vma=False
    )
```

profile of v0, /device:TPU:0, one launch (start us, length us, event | category | flops | bytes accessed | tf_op | source)
XLA Modules:
  0.0 143.7 jit_solution(14677089066934302279)
XLA Ops:
  7.2 5.7 %fusion.13 = (f32[1,1,1,3,6,4608]{5,1,4,3,2,0:T(1,128)S(1)}, f32[1,1,1,3,6,4608]{5,1,4,3,2,0:T(1,128)S(1)}, f32[1,1,1,3,6,4608]{5,1,4,3,2,0:T(1,128)S(1)}, f32[1...) fusion(f32[3,2,3,3,6,4608]{5,1,4,3,2,0:T(2,128)} %param.1), kind=kLoop, calls=%fused_computation.88 | loop fusion | bytes 7962624 | tf_op jit(solution)/shard_map/slice | solution.py:30
  12.9 3.9 %fusion.14 = (f32[1,1,3,3,6,4608]{5,1,4,3,2,0:T(1,128)S(1)}, f32[1,1,3,3,6,4608]{5,1,4,3,2,0:T(1,128)S(1)}) fusion(f32[3,2,3,3,6,4608]{5,1,4,3,2,0:T(2,128)} %param.1), kind=kLoop, calls=%fused_computation.89 | loop fusion | bytes 3981312 | tf_op jit(solution)/shard_map/slice | solution.py:28
  16.9 0.3 copy_bitcast_fusion
  17.4 0.1 copy_bitcast_fusion.8
  17.5 0.1 copy_bitcast_fusion.10
  17.8 1.0 subtract_add_fusion.4
  19.3 0.3 copy-done.1
  19.7 0.1 copy-done.2
  19.8 0.1 copy-done.3
  19.9 0.2 copy-done.4
  20.1 0.9 subtract_add_fusion.3
  21.0 1.8 %pad_maximum_fusion = f32[2,3,3,6,4608]{4,3,2,1,0:T(8,128)} fusion(f32[1,3,3,6,4608]{4,3,2,1,0:T(8,128)S(1)} %get-tuple-element.56, f32[1,3,3,6,4608]{4,3,2,1,0:T(8,128)S(1)} %get-tuple-element.55), kind=kLoop, calls=%fused_computation | loop fusion | flops 497664 | bytes 3981312 | tf_op jit(solution)/shard_map/stack | solution.py:34
  22.8 0.2 all-reduce.3.cloned.1.call-start
  23.1 2.4 %subtract_add_fusion.1 = (f32[3,3,6,4608]{3,2,1,0:T(8,128)S(1)}, f32[3,3,6,4608]{3,2,1,0:T(8,128)S(1)}) fusion(f32[3,6,4608]{2,1,0:T(8,128)S(1)} %get-tuple-element.90, f32[3,6,4608]{2,1,0:T(8,128)S(1)} %get-tuple-element.77, f32[3,6,4608]{2,1,0:T(8,128)S(1)} %get-tuple-element.91, f32[3,6,4608]{2,1,0:T(8,128)} %copy-done.3, ...), kind=kLoop, calls=%fused_computation.11 | loop fusion | flops 5474304 | bytes 5971968 | tf_op jit(solution)/shard_map/add | solution.py:36
  25.7 15.4 %all-gather.6.cloned.1.call-done = f32[4,3,3,6,4608]{4,3,2,1,0:T(8,128)} async-done(((f32[2,3,3,6,4608]{4,3,2,1,0:T(8,128)}), f32[4,3,3,6,4608]{4,3,2,1,0:T(8,128)}) %all-gather.6.cloned.1.call-update) | async-done | bytes 3981328 | tf_op jit(solution)/shard_map/all_gather | solution.py:9
  41.0 2.1 %broadcast_multiply_fusion.5 = (f32[3,6,4608]{2,1,0:T(8,128)S(1)}, f32[3,6,4608]{2,1,0:T(8,128)S(1)}, f32[3,6,4608]{2,1,0:T(8,128)S(1)}, f32[3,6,4608]{2,1,0:T(8...) fusion(f32[2,2,3,3,6,4608]{5,4,3,2,1,0:T(8,128)} %bitcast.118), kind=kLoop, calls=%fused_computation.72 | loop fusion | flops 497664 | bytes 3981312 | tf_op jit(solution)/shard_map/while/body/eval_jaxpr/mul | solution.py:32
  43.1 1.2 copy-done
  44.3 0.2 slice_bitcast_fusion.19
  44.5 0.9 subtract_add_fusion.2
  45.4 0.2 stack_broadcast_in_dim.2
  45.5 0.3 maximum_select_fusion
  45.9 0.2 slice_bitcast_fusion.1
  46.3 1.0 subtract_add_fusion
  47.2 0.8 fusion.8
  48.1 19.6 %all-reduce.3.cloned.1.call-done = f32[2,6,4608]{2,1,0:T(8,128)} async-done(((f32[2,6,4608]{2,1,0:T(8,128)}), f32[2,6,4608]{2,1,0:T(8,128)}) %all-reduce.3.cloned.1.call-update) | async-done | bytes 221200 | tf_op jit(solution)/shard_map/psum | solution.py:21
  67.7 0.9 dynamic-slice_bitcast_fusion
  68.6 0.7 copy.52
  69.3 61.6 %all-gather.4.cloned.1.call-done = f32[96,2,2304]{2,1,0:T(2,128)} async-done(((f32[6,2,2304]{2,1,0:T(2,128)}), f32[96,2,2304]{2,1,0:T(2,128)}) %all-gather.4.cloned.1.call-update) | async-done | bytes 1769488 | tf_op jit(solution)/shard_map/all_gather | solution.py:88
  131.0 2.9 %fusion.2 = f32[6,96]{1,0:T(8,128)S(1)} fusion(f32[6,2,2304]{2,0,1:T(8,128)S(1)} %dynamic-slice_bitcast_fusion, f32[96,2,2304]{2,1,0:T(2,128)} %all-gather.4.cloned.1.call-done), kind=kOutput, calls=%fused_computation.18 | convolution fusion | flops 31850496 | bytes 1882368 | tf_op jit(solution)/shard_map/dot_general | solution.py:47
  133.9 0.1 select_reduce_fusion
  134.1 2.5 %psum.15 = f32[6,49]{1,0:T(8,128)S(1)} all-reduce(f32[6,49]{1,0:T(8,128)S(1)} %select_reduce_fusion), channel_id=1, replica_groups=mesh['ta'=2,'gx'=16] {'ta'}, use_global_device_ids=true, to_apply=%region_2.3 | all-reduce | flops 294 | bytes 2352 | tf_op jit(solution)/shard_map/psum | solution.py:93
  136.5 0.6 broadcast_multiply_fusion.6
  (26 shorter events, 1.4 us)
Async XLA Ops:
  7.2 33.9 %all-gather.6.cloned.1.call-start = ((), (), s32[]{:S(2)}) async-start(), calls=%async_computation.2 | async-start | bytes 7962624 | tf_op jit(solution)/shard_map/all_gather | solution.py:9
  18.8 0.8 copy-start.1
  18.9 0.8 copy-start.2
  18.9 1.0 copy-start.3
  19.0 1.1 copy-start.4
  22.8 44.8 %all-reduce.3.cloned.1.call-start = ((), (), s32[]{:S(2)}) async-start(), calls=%async_computation | async-start | bytes 589824 | tf_op jit(solution)/shard_map/psum | solution.py:21
  41.0 3.3 %copy-start = (f32[4,3,3,6,4608]{4,3,2,1,0:T(8,128)S(1)}, f32[4,3,3,6,4608]{4,3,2,1,0:T(8,128)}, u32[]{:S(2)}) copy-start(f32[4,3,3,6,4608]{4,3,2,1,0:T(8,128)} %all-gather.6.cloned.1.call-done) | copy-start | bytes 11943940
  48.0 82.9 %all-gather.4.cloned.1.call-start = ((), (), s32[]{:S(2)}) async-start(), calls=%async_computation.1 | async-start | bytes 1880064 | tf_op jit(solution)/shard_map/all_gather | solution.py:88
Sparse Core Ops, SparseCore 0:
  22.9 18.0 all-gather.5
  48.2 19.4 all-reduce.2
  71.0 59.8 all-gather.3
where the time goes:
time: 144 us
  waiting for transfers between devices  96.6 us (67%)
  local copies, waits for them, and re-layouts  15.5 us (11%)
  between operations  14 us (10%)
  other arithmetic  11.8 us (8%)
  matrix products  2.94 us (2%)
  blocking collectives  2.47 us (2%)
    all_gather x1, waiting for transfers between devices, per_device(): shard_rows = lax.all_gather(loop_planes, 'gx', axis=0, tiled=True)  61.6 us
    psum x1, waiting for transfers between devices, spread(): return lax.psum(kept, axis)  19.6 us
    all_gather x1, waiting for transfers between devices, prefix(): pieces = lax.all_gather(value, axis)  15.4 us
    add x5, other arithmetic, complex_mul(): terms_real[0] + terms_real[1] + terms_real[2]  6.09 us
    slice x1, local copies, waits for them, and re-layouts, complex_mul(): right_real = right[0][middle:middle + 1]  5.72 us
    slice x2, local copies, waits for them, and re-layouts, complex_mul(): left_real = left[0][:, middle:middle + 1]  3.92 us
    dot_general x1, matrix products, correlation(): lax.dot_general(own_rows, others, (((1,), (1,)), ((), ())), precision=lax...  2.94 us
  transfers between devices with their start and end apart: 3, of which 3 were waited for; matrix products, arithmetic and copies ran while one was open for 2% of the time, Pallas kernels for 0%

commit v1 on v0

--- a/solution.py
+++ b/solution.py
@@ -2,6 +2,18 @@
 import jax.numpy as jnp
 from jax import lax
 from jax.sharding import PartitionSpec as P
+
+
+def search_patches_now(u_in):
+    n_parts = jax.lax.axis_size("gx")
+    history = [u_in]
+    for idx in range(n_parts - 1):
+        t1 = jax.lax.ppermute(
+            history[-1], "gx", [(nth, (nth + 1) % n_parts) for nth in range(n_parts)]
+        )
+        history.append(t1)
+    val = jnp.concatenate(history[::-1], axis=0)
+    return jnp.roll(val, shift=(jax.lax.axis_index("gx") + 1) * u_in.shape[0], axis=0)
 
 
 def prefix(value, axis, join, neutral):
@@ -85,7 +97,7 @@
     far_blocks = gx_count // 2
     longest = planes * far_blocks
     own_rows = loop_planes.reshape(planes, flat_width)
-    shard_rows = lax.all_gather(loop_planes, "gx", axis=0, tiled=True)
+    shard_rows = search_patches_now(loop_planes)
     products = correlation(own_rows, shard_rows.reshape(shard_rows.shape[0], flat_width))
     totals_part = by_separation(
         products, -lax.axis_index("gx") * planes, longest, planes * gx_count

time: 144 us -> 271 us (1.88)
  waiting for transfers between devices: 96.6 us -> 167 us
  local copies, waits for them, and re-layouts: 15.5 us -> 68.8 us
    ppermute x0 -> x15, waiting for transfers between devices: none -> 132 us  [search_patches_now(): jax.lax.ppermute(history[-1], 'gx', [(nth, (nth + 1) % n_parts) for nth i...]
    all_gather x1 -> x0, waiting for transfers between devices: 61.6 us -> none  [per_device(): shard_rows = lax.all_gather(loop_planes, 'gx', axis=0, tiled=True)]
    concatenate x0 -> x1, local copies, waits for them, and re-layouts: none -> 46.1 us  [search_patches_now(): jnp.roll(val, shift=(jax.lax.axis_index('gx') + 1) * u_in.shape[0], axis=0)]
    unnamed x11 -> x41, local copies, waits for them, and re-layouts: 2.65 us -> 9.87 us
  transfers between devices with their start and end apart: 3 -> 17, of which waited for: 3 -> 17; matrix products, arithmetic and copies ran while one was open for 2% -> 1% of each run, Pallas kernels for 0% -> 0%
where the time goes in v1:
time: 271 us; the launch traced here: 269 us
  waiting for transfers between devices  167 us (62%)
  local copies, waits for them, and re-layouts  68.8 us (25%)
  between operations  14.4 us (5%)
  other arithmetic  11.9 us (4%)
    ppermute x15, waiting for transfers between devices, search_patches_now(): jax.lax.ppermute(history[-1], 'gx', [(nth, (nth + 1) % n_parts) for nth i...  132 us
    concatenate x1, local copies, waits for them, and re-layouts, search_patches_now(): jnp.roll(val, shift=(jax.lax.axis_index('gx') + 1) * u_in.shape[0], axis=0)  46.1 us
    psum x1, waiting for transfers between devices, spread(): return lax.psum(kept, axis)  19.6 us
    all_gather x1, waiting for transfers between devices, prefix(): pieces = lax.all_gather(value, axis)  15.4 us
    unnamed x41, local copies, waits for them, and re-layouts  9.87 us
    add x5, other arithmetic, complex_mul(): terms_real[0] + terms_real[1] + terms_real[2]  6.09 us
    slice x1, local copies, waits for them, and re-layouts, complex_mul(): right_real = right[0][middle:middle + 1]  5.72 us
  transfers between devices with their start and end apart: 17, of which 17 were waited for; matrix products, arithmetic and copies ran while one was open for 1% of the time, Pallas kernels for 0%

profile of v1, /device:TPU:0, one launch (start us, length us, event | category | flops | bytes accessed | tf_op | source)
XLA Modules:
  0.0 269.1 jit_solution(10334186285682721393)
XLA Ops:
  7.2 5.7 %fusion.14 = (f32[1,1,1,3,6,4608]{5,1,4,3,2,0:T(1,128)S(1)}, f32[1,1,1,3,6,4608]{5,1,4,3,2,0:T(1,128)S(1)}, f32[1,1,1,3,6,4608]{5,1,4,3,2,0:T(1,128)S(1)}, f32[1...) fusion(f32[3,2,3,3,6,4608]{5,1,4,3,2,0:T(2,128)} %param.1), kind=kLoop, calls=%fused_computation.89 | loop fusion | bytes 7962624 | tf_op jit(solution)/shard_map/slice | solution.py:42
  12.9 3.9 %fusion.15 = (f32[1,1,3,3,6,4608]{5,1,4,3,2,0:T(1,128)S(1)}, f32[1,1,3,3,6,4608]{5,1,4,3,2,0:T(1,128)S(1)}) fusion(f32[3,2,3,3,6,4608]{5,1,4,3,2,0:T(2,128)} %param.1), kind=kLoop, calls=%fused_computation.90 | loop fusion | bytes 3981312 | tf_op jit(solution)/shard_map/slice | solution.py:40
  17.8 1.0 subtract_add_fusion.4
  20.1 0.9 subtract_add_fusion.3
  21.0 1.8 pad_maximum_fusion
  23.1 2.4 subtract_add_fusion.1
  25.7 15.4 %all-gather.3.cloned.1.call-done = f32[4,3,3,6,4608]{4,3,2,1,0:T(8,128)} async-done(((f32[2,3,3,6,4608]{4,3,2,1,0:T(8,128)}), f32[4,3,3,6,4608]{4,3,2,1,0:T(8,128)}) %all-gather.3.cloned.1.call-update) | async-done | bytes 3981328 | tf_op jit(solution)/shard_map/all_gather | solution.py:21
  41.0 2.1 broadcast_multiply_fusion.5
  43.2 1.2 copy-done
  44.5 0.9 subtract_add_fusion.2
  46.3 1.0 subtract_add_fusion
  48.1 19.6 %all-reduce.3.cloned.1.call-done = f32[2,6,4608]{2,1,0:T(8,128)} async-done(((f32[2,6,4608]{2,1,0:T(8,128)}), f32[2,6,4608]{2,1,0:T(8,128)}) %all-reduce.3.cloned.1.call-update) | async-done | bytes 221200 | tf_op jit(solution)/shard_map/psum | solution.py:33
  67.7 0.9 dynamic-slice_bitcast_fusion
  68.6 1.8 collective-permute-start
  70.5 7.9 %collective-permute-done = f32[6,2,2304]{2,0,1:T(8,128)S(1)} collective-permute-done((f32[6,2,2304]{2,0,1:T(8,128)S(1)}, f32[6,2,2304]{2,0,1:T(8,128)S(1)}, u32[]{:S(2)}, u32[]{:S(2)}) %collective-permute-start) | collective-permute-done | bytes 110624 | tf_op jit(solution)/shard_map/ppermute | solution.py:11
  79.0 8.9 %collective-permute-done.1 = f32[6,2,2304]{2,0,1:T(8,128)S(1)} collective-permute-done((f32[6,2,2304]{2,0,1:T(8,128)S(1)}, f32[6,2,2304]{2,0,1:T(8,128)S(1)}, u32[]{:S(2)}, u32[]{:S(2)}) %collective-permute-start.1) | collective-permute-done | bytes 110624 | tf_op jit(solution)/shard_map/ppermute | solution.py:11
  88.6 8.7 %collective-permute-done.2 = f32[6,2,2304]{2,0,1:T(8,128)S(1)} collective-permute-done((f32[6,2,2304]{2,0,1:T(8,128)S(1)}, f32[6,2,2304]{2,0,1:T(8,128)S(1)}, u32[]{:S(2)}, u32[]{:S(2)}) %collective-permute-start.2) | collective-permute-done | bytes 110624 | tf_op jit(solution)/shard_map/ppermute | solution.py:11
  98.0 8.7 %collective-permute-done.3 = f32[6,2,2304]{2,0,1:T(8,128)S(1)} collective-permute-done((f32[6,2,2304]{2,0,1:T(8,128)S(1)}, f32[6,2,2304]{2,0,1:T(8,128)S(1)}, u32[]{:S(2)}, u32[]{:S(2)}) %collective-permute-start.3) | collective-permute-done | bytes 110624 | tf_op jit(solution)/shard_map/ppermute | solution.py:11
  107.4 8.7 %collective-permute-done.4 = f32[6,2,2304]{2,0,1:T(8,128)S(1)} collective-permute-done((f32[6,2,2304]{2,0,1:T(8,128)S(1)}, f32[6,2,2304]{2,0,1:T(8,128)S(1)}, u32[]{:S(2)}, u32[]{:S(2)}) %collective-permute-start.4) | collective-permute-done | bytes 110624 | tf_op jit(solution)/shard_map/ppermute | solution.py:11
  116.8 8.7 %collective-permute-done.5 = f32[6,2,2304]{2,0,1:T(8,128)S(1)} collective-permute-done((f32[6,2,2304]{2,0,1:T(8,128)S(1)}, f32[6,2,2304]{2,0,1:T(8,128)S(1)}, u32[]{:S(2)}, u32[]{:S(2)}) %collective-permute-start.5) | collective-permute-done | bytes 110624 | tf_op jit(solution)/shard_map/ppermute | solution.py:11
  126.2 9.0 %collective-permute-done.6 = f32[6,2,2304]{2,0,1:T(8,128)S(1)} collective-permute-done((f32[6,2,2304]{2,0,1:T(8,128)S(1)}, f32[6,2,2304]{2,0,1:T(8,128)S(1)}, u32[]{:S(2)}, u32[]{:S(2)}) %collective-permute-start.6) | collective-permute-done | bytes 110624 | tf_op jit(solution)/shard_map/ppermute | solution.py:11
  135.8 10.1 %collective-permute-done.7 = f32[6,2,2304]{2,0,1:T(8,128)S(1)} collective-permute-done((f32[6,2,2304]{2,0,1:T(8,128)S(1)}, f32[6,2,2304]{2,0,1:T(8,128)S(1)}, u32[]{:S(2)}, u32[]{:S(2)}) %collective-permute-start.7) | collective-permute-done | bytes 110624 | tf_op jit(solution)/shard_map/ppermute | solution.py:11
  146.6 9.4 %collective-permute-done.8 = f32[6,2,2304]{2,0,1:T(8,128)S(1)} collective-permute-done((f32[6,2,2304]{2,0,1:T(8,128)S(1)}, f32[6,2,2304]{2,0,1:T(8,128)S(1)}, u32[]{:S(2)}, u32[]{:S(2)}) %collective-permute-start.8) | collective-permute-done | bytes 110624 | tf_op jit(solution)/shard_map/ppermute | solution.py:11
  156.7 8.7 %collective-permute-done.9 = f32[6,2,2304]{2,0,1:T(8,128)S(1)} collective-permute-done((f32[6,2,2304]{2,0,1:T(8,128)S(1)}, f32[6,2,2304]{2,0,1:T(8,128)S(1)}, u32[]{:S(2)}, u32[]{:S(2)}) %collective-permute-start.9) | collective-permute-done | bytes 110624 | tf_op jit(solution)/shard_map/ppermute | solution.py:11
  166.1 8.7 %collective-permute-done.10 = f32[6,2,2304]{2,0,1:T(8,128)S(1)} collective-permute-done((f32[6,2,2304]{2,0,1:T(8,128)S(1)}, f32[6,2,2304]{2,0,1:T(8,128)S(1)}, u32[]{:S(2)}, u32[]{:S(2)}) %collective-permute-start.10) | collective-permute-done | bytes 110624 | tf_op jit(solution)/shard_map/ppermute | solution.py:11
  175.5 8.7 %collective-permute-done.11 = f32[6,2,2304]{2,0,1:T(8,128)S(1)} collective-permute-done((f32[6,2,2304]{2,0,1:T(8,128)S(1)}, f32[6,2,2304]{2,0,1:T(8,128)S(1)}, u32[]{:S(2)}, u32[]{:S(2)}) %collective-permute-start.11) | collective-permute-done | bytes 110624 | tf_op jit(solution)/shard_map/ppermute | solution.py:11
  184.2 8.7 %collective-permute-done.12 = f32[6,2,2304]{2,0,1:T(8,128)S(1)} collective-permute-done((f32[6,2,2304]{2,0,1:T(8,128)S(1)}, f32[6,2,2304]{2,0,1:T(8,128)S(1)}, u32[]{:S(2)}, u32[]{:S(2)}) %collective-permute-start.12) | collective-permute-done | bytes 110624 | tf_op jit(solution)/shard_map/ppermute | solution.py:11
  193.0 8.7 %collective-permute-done.13 = f32[6,2,2304]{2,0,1:T(8,128)S(1)} collective-permute-done((f32[6,2,2304]{2,0,1:T(8,128)S(1)}, f32[6,2,2304]{2,0,1:T(8,128)S(1)}, u32[]{:S(2)}, u32[]{:S(2)}) %collective-permute-start.13) | collective-permute-done | bytes 110624 | tf_op jit(solution)/shard_map/ppermute | solution.py:11
  202.5 8.1 %collective-permute-done.14 = f32[6,2,2304]{2,0,1:T(8,128)} collective-permute-done((f32[6,2,2304]{2,0,1:T(8,128)S(1)}, f32[6,2,2304]{2,0,1:T(8,128)}, u32[]{:S(2)}, u32[]{:S(2)}) %collective-permute-start.14) | collective-permute-done | bytes 110624 | tf_op jit(solution)/shard_map/ppermute | solution.py:11
  210.6 46.1 %concatenate.6 = f32[192,2,2304]{2,0,1:T(8,128)S(1)} concatenate(f32[6,2,2304]{2,0,1:T(8,128)} %collective-permute-done.14, f32[6,2,2304]{2,0,1:T(8,128)} %copy-done.19, f32[6,2,2304]{2,0,1:T(8,128)} %copy-done.18, f32[6,2,2304]{2,0,1:T(8,128)} %copy-done.17, f32[6,2,2304]{2,0,1:T(8,128)} %copy-done.16, f32[6,2,2304]{2,0,1:T(8,128)} %copy-done.15, f32[6,2,2304]{2,0,1:T(8,128)} %copy-done.14, ...), dimensions={0} | concatenate | bytes 7077888 | tf_op jit(solution)/shard_map/jit(_roll_dynamic)/concatenate | solution.py:16
  256.6 2.4 fusion.2
  259.2 2.5 psum.15
  (84 shorter events, 13.2 us)
Async XLA Ops:
  7.2 33.9 %all-gather.3.cloned.1.call-start = ((), (), s32[]{:S(2)}) async-start(), calls=%async_computation.1 | async-start | bytes 7962624 | tf_op jit(solution)/shard_map/all_gather | solution.py:21
  18.8 0.8 copy-start.1
  18.9 0.8 copy-start.2
  18.9 1.0 copy-start.3
  19.0 1.1 copy-start.4
  22.8 44.8 %all-reduce.3.cloned.1.call-start = ((), (), s32[]{:S(2)}) async-start(), calls=%async_computation | async-start | bytes 589824 | tf_op jit(solution)/shard_map/psum | solution.py:33
  41.0 3.3 %copy-start = (f32[4,3,3,6,4608]{4,3,2,1,0:T(8,128)S(1)}, f32[4,3,3,6,4608]{4,3,2,1,0:T(8,128)}, u32[]{:S(2)}) copy-start(f32[4,3,3,6,4608]{4,3,2,1,0:T(8,128)} %all-gather.3.cloned.1.call-done) | copy-start | bytes 11943940
  68.6 133.8 %copy-start.5 = (f32[6,2,2304]{2,0,1:T(8,128)}, f32[6,2,2304]{2,0,1:T(8,128)S(1)}, u32[]{:S(2)}) copy-start(f32[6,2,2304]{2,0,1:T(8,128)S(1)} %dynamic-slice_bitcast_fusion) | copy-start | bytes 331780
  68.6 9.8 %collective-permute-start = (f32[6,2,2304]{2,0,1:T(8,128)S(1)}, f32[6,2,2304]{2,0,1:T(8,128)S(1)}, u32[]{:S(2)}, u32[]{:S(2)}) collective-permute-start(f32[6,2,2304]{2,0,1:T(8,128)S(1)} %dynamic-slice_bitcast_fusion), channel_id=1, source_target_pairs={{0,1},{1,2},{2,3},{3,4},{4,5},{5,6},{6,7},{7,8},{8,9},{9,10},{10,1... | collective-permute-start | bytes 331784 | tf_op jit(solution)/shard_map/ppermute | solution.py:11
  79.0 8.9 %collective-permute-start.1 = (f32[6,2,2304]{2,0,1:T(8,128)S(1)}, f32[6,2,2304]{2,0,1:T(8,128)S(1)}, u32[]{:S(2)}, u32[]{:S(2)}) collective-permute-start(f32[6,2,2304]{2,0,1:T(8,128)S(1)} %collective-permute-done), channel_id=1, source_target_pairs={{0,1},{1,2},{2,3},{3,4},{4,5},{5,6},{6,7},{7,8},{8,9},{9,10},{10,1... | collective-permute-start | bytes 331784 | tf_op jit(solution)/shard_map/ppermute | solution.py:11
  87.9 0.7 copy-start.7
  88.6 8.7 %collective-permute-start.2 = (f32[6,2,2304]{2,0,1:T(8,128)S(1)}, f32[6,2,2304]{2,0,1:T(8,128)S(1)}, u32[]{:S(2)}, u32[]{:S(2)}) collective-permute-start(f32[6,2,2304]{2,0,1:T(8,128)S(1)} %collective-permute-done.1), channel_id=1, source_target_pairs={{0,1},{1,2},{2,3},{3,4},{4,5},{5,6},{6,7},{7,8},{8,9},{9,10},{10,1... | collective-permute-start | bytes 331784 | tf_op jit(solution)/shard_map/ppermute | solution.py:11
  97.3 0.7 copy-start.8
  98.0 8.7 %collective-permute-start.3 = (f32[6,2,2304]{2,0,1:T(8,128)S(1)}, f32[6,2,2304]{2,0,1:T(8,128)S(1)}, u32[]{:S(2)}, u32[]{:S(2)}) collective-permute-start(f32[6,2,2304]{2,0,1:T(8,128)S(1)} %collective-permute-done.2), channel_id=1, source_target_pairs={{0,1},{1,2},{2,3},{3,4},{4,5},{5,6},{6,7},{7,8},{8,9},{9,10},{10,1... | collective-permute-start | bytes 331784 | tf_op jit(solution)/shard_map/ppermute | solution.py:11
  106.7 0.7 copy-start.9
  107.4 8.7 %collective-permute-start.4 = (f32[6,2,2304]{2,0,1:T(8,128)S(1)}, f32[6,2,2304]{2,0,1:T(8,128)S(1)}, u32[]{:S(2)}, u32[]{:S(2)}) collective-permute-start(f32[6,2,2304]{2,0,1:T(8,128)S(1)} %collective-permute-done.3), channel_id=1, source_target_pairs={{0,1},{1,2},{2,3},{3,4},{4,5},{5,6},{6,7},{7,8},{8,9},{9,10},{10,1... | collective-permute-start | bytes 331784 | tf_op jit(solution)/shard_map/ppermute | solution.py:11
  116.8 8.7 %collective-permute-start.5 = (f32[6,2,2304]{2,0,1:T(8,128)S(1)}, f32[6,2,2304]{2,0,1:T(8,128)S(1)}, u32[]{:S(2)}, u32[]{:S(2)}) collective-permute-start(f32[6,2,2304]{2,0,1:T(8,128)S(1)} %collective-permute-done.4), channel_id=1, source_target_pairs={{0,1},{1,2},{2,3},{3,4},{4,5},{5,6},{6,7},{7,8},{8,9},{9,10},{10,1... | collective-permute-start | bytes 331784 | tf_op jit(solution)/shard_map/ppermute | solution.py:11
  125.5 0.7 copy-start.11
  126.2 9.0 %collective-permute-start.6 = (f32[6,2,2304]{2,0,1:T(8,128)S(1)}, f32[6,2,2304]{2,0,1:T(8,128)S(1)}, u32[]{:S(2)}, u32[]{:S(2)}) collective-permute-start(f32[6,2,2304]{2,0,1:T(8,128)S(1)} %collective-permute-done.5), channel_id=1, source_target_pairs={{0,1},{1,2},{2,3},{3,4},{4,5},{5,6},{6,7},{7,8},{8,9},{9,10},{10,1... | collective-permute-start | bytes 331784 | tf_op jit(solution)/shard_map/ppermute | solution.py:11
  135.8 10.1 %collective-permute-start.7 = (f32[6,2,2304]{2,0,1:T(8,128)S(1)}, f32[6,2,2304]{2,0,1:T(8,128)S(1)}, u32[]{:S(2)}, u32[]{:S(2)}) collective-permute-start(f32[6,2,2304]{2,0,1:T(8,128)S(1)} %collective-permute-done.6), channel_id=1, source_target_pairs={{0,1},{1,2},{2,3},{3,4},{4,5},{5,6},{6,7},{7,8},{8,9},{9,10},{10,1... | collective-permute-start | bytes 331784 | tf_op jit(solution)/shard_map/ppermute | solution.py:11
  145.9 0.7 copy-start.13
  146.6 9.4 %collective-permute-start.8 = (f32[6,2,2304]{2,0,1:T(8,128)S(1)}, f32[6,2,2304]{2,0,1:T(8,128)S(1)}, u32[]{:S(2)}, u32[]{:S(2)}) collective-permute-start(f32[6,2,2304]{2,0,1:T(8,128)S(1)} %collective-permute-done.7), channel_id=1, source_target_pairs={{0,1},{1,2},{2,3},{3,4},{4,5},{5,6},{6,7},{7,8},{8,9},{9,10},{10,1... | collective-permute-start | bytes 331784 | tf_op jit(solution)/shard_map/ppermute | solution.py:11
  156.7 8.7 %collective-permute-start.9 = (f32[6,2,2304]{2,0,1:T(8,128)S(1)}, f32[6,2,2304]{2,0,1:T(8,128)S(1)}, u32[]{:S(2)}, u32[]{:S(2)}) collective-permute-start(f32[6,2,2304]{2,0,1:T(8,128)S(1)} %collective-permute-done.8), channel_id=1, source_target_pairs={{0,1},{1,2},{2,3},{3,4},{4,5},{5,6},{6,7},{7,8},{8,9},{9,10},{10,1... | collective-permute-start | bytes 331784 | tf_op jit(solution)/shard_map/ppermute | solution.py:11
  166.1 8.7 %collective-permute-start.10 = (f32[6,2,2304]{2,0,1:T(8,128)S(1)}, f32[6,2,2304]{2,0,1:T(8,128)S(1)}, u32[]{:S(2)}, u32[]{:S(2)}) collective-permute-start(f32[6,2,2304]{2,0,1:T(8,128)S(1)} %collective-permute-done.9), channel_id=1, source_target_pairs={{0,1},{1,2},{2,3},{3,4},{4,5},{5,6},{6,7},{7,8},{8,9},{9,10},{10,1... | collective-permute-start | bytes 331784 | tf_op jit(solution)/shard_map/ppermute | solution.py:11
  174.8 0.7 copy-start.16
  175.5 8.7 %collective-permute-start.11 = (f32[6,2,2304]{2,0,1:T(8,128)S(1)}, f32[6,2,2304]{2,0,1:T(8,128)S(1)}, u32[]{:S(2)}, u32[]{:S(2)}) collective-permute-start(f32[6,2,2304]{2,0,1:T(8,128)S(1)} %collective-permute-done.10), channel_id=1, source_target_pairs={{0,1},{1,2},{2,3},{3,4},{4,5},{5,6},{6,7},{7,8},{8,9},{9,10},{10,1... | collective-permute-start | bytes 331784 | tf_op jit(solution)/shard_map/ppermute | solution.py:11
  184.2 18.2 %copy-start.17 = (f32[6,2,2304]{2,0,1:T(8,128)}, f32[6,2,2304]{2,0,1:T(8,128)S(1)}, u32[]{:S(2)}) copy-start(f32[6,2,2304]{2,0,1:T(8,128)S(1)} %collective-permute-done.11) | copy-start | bytes 331780
  184.2 8.7 %collective-permute-start.12 = (f32[6,2,2304]{2,0,1:T(8,128)S(1)}, f32[6,2,2304]{2,0,1:T(8,128)S(1)}, u32[]{:S(2)}, u32[]{:S(2)}) collective-permute-start(f32[6,2,2304]{2,0,1:T(8,128)S(1)} %collective-permute-done.11), channel_id=1, source_target_pairs={{0,1},{1,2},{2,3},{3,4},{4,5},{5,6},{6,7},{7,8},{8,9},{9,10},{10,1... | collective-permute-start | bytes 331784 | tf_op jit(solution)/shard_map/ppermute | solution.py:11
  193.0 9.5 %copy-start.18 = (f32[6,2,2304]{2,0,1:T(8,128)}, f32[6,2,2304]{2,0,1:T(8,128)S(1)}, u32[]{:S(2)}) copy-start(f32[6,2,2304]{2,0,1:T(8,128)S(1)} %collective-permute-done.12) | copy-start | bytes 331780
  193.0 8.7 %collective-permute-start.13 = (f32[6,2,2304]{2,0,1:T(8,128)S(1)}, f32[6,2,2304]{2,0,1:T(8,128)S(1)}, u32[]{:S(2)}, u32[]{:S(2)}) collective-permute-start(f32[6,2,2304]{2,0,1:T(8,128)S(1)} %collective-permute-done.12), channel_id=1, source_target_pairs={{0,1},{1,2},{2,3},{3,4},{4,5},{5,6},{6,7},{7,8},{8,9},{9,10},{10,1... | collective-permute-start | bytes 331784 | tf_op jit(solution)/shard_map/ppermute | solution.py:11
  201.7 0.8 copy-start.19
  201.7 8.8 %collective-permute-start.14 = (f32[6,2,2304]{2,0,1:T(8,128)S(1)}, f32[6,2,2304]{2,0,1:T(8,128)}, u32[]{:S(2)}, u32[]{:S(2)}) collective-permute-start(f32[6,2,2304]{2,0,1:T(8,128)S(1)} %collective-permute-done.13), channel_id=1, source_target_pairs={{0,1},{1,2},{2,3},{3,4},{4,5},{5,6},{6,7},{7,8},{8,9},{9,10},{10,1... | collective-permute-start | bytes 331784 | tf_op jit(solution)/shard_map/ppermute | solution.py:11
  (5 other events, 3.2 us)
Sparse Core Ops, SparseCore 0:
  23.0 18.0 all-gather.2
  48.2 19.4 all-reduce.2
